TPU v7x, 32 devices: a whole 2x2x4 slice. The times are simulated.
32 devices in a mesh: owner: 8 (over z, core), sub: 4 (over y, x).
Axes of the slice: x: 2, y: 2, z: 4, core: 2. Of those that a mesh axis runs over, the one named last changes fastest.
Arguments:
- residual: float32 [256, 4608], P('owner', 'sub'), may hold values from -6 to 6
- counts: int32 [8, 16], P('owner', 'sub'), may hold values from 1 to 36
- assembly: int32 [8, 16, 36, 2304], P('owner', 'sub'), may hold values from 0 to 1, as said below
- level_two: float32 [8, 2304, 2304], P('owner', 'sub'), as said below
- block_inverse: float32 [8, 2304, 144], P('owner', 'sub'), as said below
Outputs:
- corrections: float32 [256, 4608], P('owner', 'sub')
- level_residual: float32 [8, 2304, 256], P('owner', 'sub')
Inputs may be any that keep to these rules, and one draw needn't show every extreme that they name: `assembly`: every row of each [36, 2304] block holds exactly one 1; split the 2304 columns into 4 equal ranges and a group's positions into runs of 4: the 144 rows of one run (live or not) put at most 72 of their 1s into one range, and in every run some range gets exactly 72. `level_two`: each group's matrix is symmetric positive definite. `block_inverse`: each diagonal block is symmetric positive definite.
All inputs are finite; a program needn't handle non-finite values.
Results may differ from a plain program's by a relative error of at most 0.0003.
Values sent between devices are 32-bit elements; how exact they have to be, the bound alone decides.
A program may use at most 64 MiB of HBM per device.

v0:
```python
import jax
import jax.numpy as jnp
from jax import lax
from jax.sharding import PartitionSpec as P

ITERS = 4


def column_sum(left, right):
    return jnp.sum(left * right, axis=0)


def shards(residual, counts, assembly, level_two, block_inverse):
    highest = lax.Precision.HIGHEST
    rows_here = level_two.shape[1]
    width = level_two.shape[2]
    block = block_inverse.shape[2]
    slots = assembly.shape[1]
    prim = assembly.shape[2]
    rows_local = slots * prim
    local = lax.all_to_all(residual, "owner", split_axis=1, concat_axis=0, tiled=True)
    live = (lax.broadcasted_iota(jnp.int32, (slots, prim), 1) < counts[0][:, None]).astype(
        jnp.float32
    )
    live_flat = live.reshape(rows_local)
    nsub = lax.axis_size("sub")
    capacity = max(2 * rows_local // nsub, 1)
    total_slots = nsub * capacity
    flat = assembly[0].reshape(rows_local, width)
    target = jnp.sum(flat * lax.broadcasted_iota(jnp.int32, (rows_local, width), 1), axis=1)
    holder = target // rows_here
    offset = target - holder * rows_here
    same = holder[:, None] == holder[None, :]
    earlier = lax.broadcasted_iota(jnp.int32, (rows_local, rows_local), 0) > lax.broadcasted_iota(
        jnp.int32, (rows_local, rows_local), 1
    )
    rank = jnp.sum((same & earlier).astype(jnp.int32), axis=1)
    place = holder * capacity + rank
    pick = (place[:, None] == lax.broadcasted_iota(jnp.int32, (rows_local, total_slots), 1)).astype(
        jnp.float32
    )
    pick_live = pick * live_flat[:, None]
    send_vals = lax.dot_general(
        pick_live,
        local,
        (((0,), (1,)), ((), ())),
        precision=highest,
        preferred_element_type=jnp.float32,
    )
    used = jnp.sum(pick, axis=0)
    send_off = (
        jnp.dot(
            offset.astype(jnp.float32), pick, precision=highest, preferred_element_type=jnp.float32
        )
        + (1.0 - used) * rows_here
    )
    recv_vals, recv_off = (
        lax.all_to_all(send_vals, "sub", split_axis=0, concat_axis=0, tiled=True),
        lax.all_to_all(send_off, "sub", split_axis=0, concat_axis=0, tiled=True),
    )
    landing = (
        recv_off.astype(jnp.int32)[:, None]
        == lax.broadcasted_iota(jnp.int32, (total_slots, rows_here), 1)
    ).astype(jnp.float32)
    level_rhs = lax.dot_general(
        landing,
        recv_vals,
        (((0,), (0,)), ((), ())),
        precision=highest,
        preferred_element_type=jnp.float32,
    )
    matrix = level_two[0]
    inverse = block_inverse[0].reshape(rows_here // block, block, block)

    def precond(vector):
        shaped = vector.reshape(rows_here // block, block, vector.shape[1])
        return jnp.einsum("bij,bjr->bir", inverse, shaped, precision=highest).reshape(
            rows_here, vector.shape[1]
        )

    def global_norm(resid, zvec):
        return lax.psum(column_sum(resid, zvec), "sub")

    solution = jnp.zeros_like(level_rhs)
    resid = level_rhs
    zvec = precond(resid)
    direction = zvec
    rz_now = global_norm(resid, zvec)
    for step in range(ITERS):
        image = jnp.dot(
            matrix,
            lax.all_gather(direction, "sub", axis=0, tiled=True),
            precision=highest,
            preferred_element_type=jnp.float32,
        )
        alpha = rz_now / lax.psum(column_sum(direction, image), "sub")
        solution = solution + alpha * direction
        resid = resid - alpha * image
        zvec = precond(resid)
        rz_next = global_norm(resid, zvec)
        direction = zvec + rz_next / rz_now * direction
        rz_now = rz_next
    reply = jnp.dot(landing, solution, precision=highest, preferred_element_type=jnp.float32)
    returned = lax.all_to_all(reply, "sub", split_axis=0, concat_axis=0, tiled=True)
    gathered = lax.dot_general(
        returned,
        pick_live,
        (((0,), (1,)), ((), ())),
        precision=highest,
        preferred_element_type=jnp.float32,
    )
    corrections = lax.all_to_all(gathered, "owner", split_axis=0, concat_axis=1, tiled=True)
    return (corrections, resid[None])


def solution(mesh):
    in_specs = (
        P("owner", "sub"),
        P("owner", "sub"),
        P("owner", "sub", None, None),
        P("owner", "sub", None),
        P("owner", "sub", None),
    )
    out_specs = (P("owner", "sub"), P("owner", "sub", None))
    return jax.shard_map(shards, mesh=mesh, in_specs=in_specs, out_specs=out_specs, check_vma=False)
```

profile of v0, /device:TPU:0, one launch (start us, length us, event | category | flops | bytes accessed | tf_op | source)
XLA Modules:
  0.0 333.1 jit_solution(15403956645179960707)
XLA Ops:
  7.2 1.2 all_to_all.46
  8.4 0.8 copy.39
  9.2 6.4 %all-to-all-start.1 = ((f32[32,8,144]{2,0,1:T(8,128)}), f32[32,8,144]{2,0,1:T(8,128)S(1)}, u32[]{:S(2)}, u32[]{:S(2)}) async-start(f32[32,8,144]{2,0,1:T(8,128)} %copy.39), calls=%async_computation.1 | async-start | bytes 524288 | tf_op jit(solution)/shard_map/all_to_all | solution.py:21
  15.5 0.7 fusion.48
  16.4 0.7 multiply_reduce_fusion
  17.9 0.7 all_to_all.44
  18.5 6.7 %all-to-all-done.1 = f32[32,8,144]{2,0,1:T(8,128)S(1)} async-done(((f32[32,8,144]{2,0,1:T(8,128)}), f32[32,8,144]{2,0,1:T(8,128)S(1)}, u32[]{:S(2)}, u32[]{:S(2)}) %all-to-all-start.1) | async-done | bytes 147488 | tf_op jit(solution)/shard_map/all_to_all | solution.py:21
  25.3 3.7 %all-to-all-start = ((f32[4,72,1]{1,2,0:T(1,128)}), f32[4,72,1]{1,2,0:T(1,128)S(1)}, u32[]{:S(2)}, u32[]{:S(2)}) async-start(f32[4,72,1]{1,2,0:T(1,128)} %all_to_all.44), calls=%async_computation | async-start | bytes 4096 | tf_op jit(solution)/shard_map/all_to_all | solution.py:59
  29.0 1.2 fusion.33
  30.1 3.4 %all-to-all-done = f32[4,72,1]{1,2,0:T(1,128)S(1)} async-done(((f32[4,72,1]{1,2,0:T(1,128)}), f32[4,72,1]{1,2,0:T(1,128)S(1)}, u32[]{:S(2)}, u32[]{:S(2)}) %all-to-all-start) | async-done | bytes 1184 | tf_op jit(solution)/shard_map/all_to_all | solution.py:59
  33.6 3.5 %all-to-all-start.2 = ((f32[4,72,256]{2,1,0:T(8,128)}), f32[4,72,256]{2,1,0:T(8,128)S(1)}, u32[]{:S(2)}, u32[]{:S(2)}) async-start(f32[4,72,256]{2,1,0:T(8,128)} %fusion.33), calls=%async_computation.2 | async-start | bytes 589824 | tf_op jit(solution)/shard_map/all_to_all | solution.py:58
  37.4 5.0 %all-to-all-done.2 = f32[4,72,256]{2,1,0:T(8,128)S(1)} async-done(((f32[4,72,256]{2,1,0:T(8,128)}), f32[4,72,256]{2,1,0:T(8,128)S(1)}, u32[]{:S(2)}, u32[]{:S(2)}) %all-to-all-start.2) | async-done | bytes 294944 | tf_op jit(solution)/shard_map/all_to_all | solution.py:58
  42.5 1.0 fusion.23
  43.5 1.5 fusion.51
  45.1 35.3 %all-gather.5.cloned.1.call-done = f32[2304,256]{1,0:T(8,128)} async-done(((f32[576,256]{1,0:T(8,128)}), f32[2304,256]{1,0:T(8,128)}) %all-gather.5.cloned.1.call-update) | async-done | bytes 2359312 | tf_op jit(solution)/shard_map/all_gather | solution.py:92
  80.4 7.7 %multiply_reduce_fusion.4 = (f32[256]{0:T(256)S(1)}, f32[256]{0:T(256)S(1)}, f32[576,256]{1,0:T(8,128)S(1)}) fusion(f32[4,256,144]{1,2,0:T(8,128)} %fusion.51, f32[576,256]{1,0:T(8,128)S(1)} %fusion.23, f32[2304,256]{1,0:T(8,128)} %all-gather.5.cloned.1.call-done, f32[1,576,2304]{2,1,0:T(8,128)} %param.8), kind=kOutput, calls=%fused_computation.44 | convolution fusion | flops 4077452800 | bytes 9439232 | tf_op jit(solution)/shard_map/dot_general | solution.py:90
  88.1 8.9 %all-reduce = (f32[256]{0:T(256)S(1)}, f32[256]{0:T(256)S(1)}) all-reduce(f32[256]{0:T(256)S(1)} %get-tuple-element.3, f32[256]{0:T(256)S(1)} %get-tuple-element.2), channel_id=1, replica_groups=mesh['owner'=8,'sub'=4] {'sub'}, use_global_device_ids=true, to_apply=%region_4.5 | all-reduce | flops 512 | bytes 4096 | tf_op jit(solution)/shard_map/psum | solution.py:82
  97.1 0.7 fusion.52
  97.9 8.9 %psum.58 = f32[256]{0:T(256)S(1)} all-reduce(f32[256]{0:T(256)S(1)} %fusion.28), channel_id=1, replica_groups=mesh['owner'=8,'sub'=4] {'sub'}, use_global_device_ids=true, to_apply=%region_8.9 | all-reduce | flops 256 | bytes 2048 | tf_op jit(solution)/shard_map/psum | solution.py:82
  106.8 0.9 bitcast_add_fusion.4
  108.0 37.3 %all-gather.7.cloned.1.call-done = f32[2304,256]{1,0:T(8,128)} async-done(((f32[576,256]{1,0:T(8,128)}), f32[2304,256]{1,0:T(8,128)}) %all-gather.7.cloned.1.call-update) | async-done | bytes 2359312 | tf_op jit(solution)/shard_map/all_gather | solution.py:92
  145.2 8.5 %multiply_reduce_fusion.3 = (f32[256]{0:T(256)S(1)}, f32[576,256]{1,0:T(8,128)}) fusion(f32[576,256]{1,0:T(8,128)} %bitcast_add_fusion.4, f32[2304,256]{1,0:T(8,128)} %all-gather.7.cloned.1.call-done, f32[1,576,2304]{2,1,0:T(8,128)} %param.8), kind=kOutput, calls=%fused_computation.42 | convolution fusion | flops 4077158144 | bytes 8848384 | tf_op jit(solution)/shard_map/dot_general | solution.py:90
  153.7 8.9 %psum.59 = f32[256]{0:T(256)S(1)} all-reduce(f32[256]{0:T(256)S(1)} %get-tuple-element.9), channel_id=1, replica_groups=mesh['owner'=8,'sub'=4] {'sub'}, use_global_device_ids=true, to_apply=%region_10.11 | all-reduce | flops 256 | bytes 2048 | tf_op jit(solution)/shard_map/psum | solution.py:96
  162.6 1.2 multiply_subtract_fusion.1
  163.8 0.7 fusion.53
  164.6 0.7 fusion.27
  165.3 9.0 %psum.60 = f32[256]{0:T(256)S(1)} all-reduce(f32[256]{0:T(256)} %fusion.27), channel_id=1, replica_groups=mesh['owner'=8,'sub'=4] {'sub'}, use_global_device_ids=true, to_apply=%region_12.13 | all-reduce | flops 256 | bytes 2048 | tf_op jit(solution)/shard_map/psum | solution.py:82
  174.9 0.9 bitcast_add_fusion.2
  175.8 37.4 %all-gather.9.cloned.1.call-done = f32[2304,256]{1,0:T(8,128)} async-done(((f32[576,256]{1,0:T(8,128)}), f32[2304,256]{1,0:T(8,128)}) %all-gather.9.cloned.1.call-update) | async-done | bytes 2359312 | tf_op jit(solution)/shard_map/all_gather | solution.py:92
  213.3 8.5 %multiply_reduce_fusion.2 = (f32[256]{0:T(256)S(1)}, f32[576,256]{1,0:T(8,128)}) fusion(f32[576,256]{1,0:T(8,128)} %bitcast_add_fusion.2, f32[2304,256]{1,0:T(8,128)} %all-gather.9.cloned.1.call-done, f32[1,576,2304]{2,1,0:T(8,128)} %param.8), kind=kOutput, calls=%fused_computation.40 | convolution fusion | flops 4077158144 | bytes 8848384 | tf_op jit(solution)/shard_map/dot_general | solution.py:90
  221.8 8.9 %psum.61 = f32[256]{0:T(256)S(1)} all-reduce(f32[256]{0:T(256)S(1)} %get-tuple-element.11), channel_id=1, replica_groups=mesh['owner'=8,'sub'=4] {'sub'}, use_global_device_ids=true, to_apply=%region_14.15 | all-reduce | flops 256 | bytes 2048 | tf_op jit(solution)/shard_map/psum | solution.py:96
  230.7 1.2 multiply_subtract_fusion
  231.9 0.7 fusion.54
  232.7 9.1 %psum.62 = f32[256]{0:T(256)S(1)} all-reduce(f32[256]{0:T(256)S(1)} %fusion.24), channel_id=1, replica_groups=mesh['owner'=8,'sub'=4] {'sub'}, use_global_device_ids=true, to_apply=%region_16.17 | all-reduce | flops 256 | bytes 2048 | tf_op jit(solution)/shard_map/psum | solution.py:82
  241.8 0.9 bitcast_add_fusion
  242.8 0.6 convert_element_type.37
  243.4 36.9 %all-gather.11.cloned.1.call-done = f32[2304,256]{1,0:T(8,128)} async-done(((f32[576,256]{1,0:T(8,128)}), f32[2304,256]{1,0:T(8,128)}) %all-gather.11.cloned.1.call-update) | async-done | bytes 2359312 | tf_op jit(solution)/shard_map/all_gather | solution.py:92
  280.3 8.2 %multiply_reduce_fusion.1 = (f32[256]{0:T(256)}, f32[576,256]{1,0:T(8,128)S(1)}) fusion(f32[576,256]{1,0:T(8,128)} %bitcast_add_fusion, f32[2304,256]{1,0:T(8,128)} %all-gather.11.cloned.1.call-done, f32[1,576,2304]{2,1,0:T(8,128)} %param.8), kind=kOutput, calls=%fused_computation.38 | convolution fusion | flops 4077158144 | bytes 8848384 | tf_op jit(solution)/shard_map/dot_general | solution.py:90
  288.5 9.6 %psum.63 = f32[256]{0:T(256)} all-reduce(f32[256]{0:T(256)} %get-tuple-element.13), channel_id=1, replica_groups=mesh['owner'=8,'sub'=4] {'sub'}, use_global_device_ids=true, to_apply=%region_18.19 | all-reduce | flops 256 | bytes 2048 | tf_op jit(solution)/shard_map/psum | solution.py:96
  298.1 0.7 div.45
  298.8 1.0 fusion.26
  299.8 1.3 fusion.21
  301.1 8.7 %all_to_all.62 = f32[4,72,256]{2,1,0:T(8,128)S(1)} all-to-all(f32[4,72,256]{2,1,0:T(8,128)S(1)} %fusion.21), channel_id=1, replica_groups=mesh['owner'=8,'sub'=4] {'sub'}, dimensions={0} | all-to-all | bytes 589824 | tf_op jit(solution)/shard_map/all_to_all | solution.py:104
  310.0 1.4 fusion.36
  311.3 4.6 %all-to-all-start.4 = ((f32[8,32,144]{2,1,0:T(8,128)}), f32[8,32,144]{2,1,0:T(8,128)S(1)}, u32[]{:S(2)}, u32[]{:S(2)}) async-start(f32[8,32,144]{2,1,0:T(8,128)} %fusion.36), calls=%async_computation.4 | async-start | bytes 524288 | tf_op jit(solution)/shard_map/all_to_all | solution.py:112
  315.9 1.5 subtract_bitcast_fusion
  317.4 8.2 %all-to-all-done.4 = f32[8,32,144]{2,1,0:T(8,128)S(1)} async-done(((f32[8,32,144]{2,1,0:T(8,128)}), f32[8,32,144]{2,1,0:T(8,128)S(1)}, u32[]{:S(2)}, u32[]{:S(2)}) %all-to-all-start.4) | async-done | bytes 147488 | tf_op jit(solution)/shard_map/all_to_all | solution.py:112
  325.8 0.8 all_to_all.56
  (76 shorter events, 2.9 us)
Async XLA Ops:
  7.2 9.2 %copy-start.7 = (s32[1,4,36,2304]{3,1,2,0:T(4,128)S(1)}, s32[1,4,36,2304]{3,1,2,0:T(4,128)}, u32[]{:S(2)}) copy-start(s32[1,4,36,2304]{3,1,2,0:T(4,128)} %param.7) | copy-start | bytes 3981316
  7.2 29.9 %copy-start.8 = (f32[1,576,144]{1,2,0:T(8,128)S(1)}, f32[1,576,144]{1,2,0:T(8,128)}, u32[]{:S(2)}) copy-start(f32[1,576,144]{1,2,0:T(8,128)} %param.9) | copy-start | bytes 995332
  9.2 16.1 %all-to-all-start.1 = ((f32[32,8,144]{2,0,1:T(8,128)}), f32[32,8,144]{2,0,1:T(8,128)S(1)}, u32[]{:S(2)}, u32[]{:S(2)}) async-start(f32[32,8,144]{2,0,1:T(8,128)} %copy.39), calls=%async_computation.1 | async-start | bytes 524288 | tf_op jit(solution)/shard_map/all_to_all | solution.py:21
  16.4 20.7 %copy-start.9 = (f32[144]{0:T(256)}, f32[144]{0:T(256)S(1)}, u32[]{:S(2)}) copy-start(f32[144]{0:T(256)S(1)} %reshape.211) | copy-start | bytes 1732
  25.3 8.3 %all-to-all-start = ((f32[4,72,1]{1,2,0:T(1,128)}), f32[4,72,1]{1,2,0:T(1,128)S(1)}, u32[]{:S(2)}, u32[]{:S(2)}) async-start(f32[4,72,1]{1,2,0:T(1,128)} %all_to_all.44), calls=%async_computation | async-start | bytes 4096 | tf_op jit(solution)/shard_map/all_to_all | solution.py:59
  33.6 8.9 %all-to-all-start.2 = ((f32[4,72,256]{2,1,0:T(8,128)}), f32[4,72,256]{2,1,0:T(8,128)S(1)}, u32[]{:S(2)}, u32[]{:S(2)}) async-start(f32[4,72,256]{2,1,0:T(8,128)} %fusion.33), calls=%async_computation.2 | async-start | bytes 589824 | tf_op jit(solution)/shard_map/all_to_all | solution.py:58
  37.0 43.4 %all-gather.5.cloned.1.call-start = ((), (), s32[]{:S(2)}) async-start(), calls=%async_computation.5 | async-start | bytes 2949120 | tf_op jit(solution)/shard_map/all_gather | solution.py:92
  45.0 100.2 %all-gather.7.cloned.1.call-start = ((), (), s32[]{:S(2)}) async-start(), calls=%async_computation.6 | async-start | bytes 2949120 | tf_op jit(solution)/shard_map/all_gather | solution.py:92
  97.0 0.9 copy-start.11
  97.0 9.8 %copy-start = (f32[4,256,144]{1,2,0:T(8,128)S(1)}, f32[4,256,144]{1,2,0:T(8,128)}, u32[]{:S(2)}) copy-start(f32[4,256,144]{1,2,0:T(8,128)} %fusion.51) | copy-start | bytes 1769476
  106.8 46.9 %copy-start.13 = (f32[256]{0:T(256)}, f32[256]{0:T(256)S(1)}, u32[]{:S(2)}) copy-start(f32[256]{0:T(256)S(1)} %div.40) | copy-start | bytes 3076
  107.7 105.6 %all-gather.9.cloned.1.call-start = ((), (), s32[]{:S(2)}) async-start(), calls=%async_computation.7 | async-start | bytes 2949120 | tf_op jit(solution)/shard_map/all_gather | solution.py:92
  162.6 1.9 copy-start.15
  162.6 12.2 %copy-start.2 = (f32[576,256]{1,0:T(8,128)S(1)}, f32[576,256]{1,0:T(8,128)}, u32[]{:S(2)}) copy-start(f32[576,256]{1,0:T(8,128)} %bitcast_add_fusion.4) | copy-start | bytes 1769476
  164.6 57.2 %copy-start.3 = (f32[4,256,144]{1,2,0:T(8,128)}, f32[4,256,144]{1,2,0:T(8,128)S(1)}, u32[]{:S(2)}) copy-start(f32[4,256,144]{1,2,0:T(8,128)S(1)} %fusion.53) | copy-start | bytes 1769476
  174.3 0.6 copy-start.16
  175.8 104.5 %all-gather.11.cloned.1.call-start = ((), (), s32[]{:S(2)}) async-start(), calls=%async_computation.8 | async-start | bytes 2949120 | tf_op jit(solution)/shard_map/all_gather | solution.py:92
  230.7 1.9 copy-start.17
  230.7 11.1 %copy-start.1 = (f32[576,256]{1,0:T(8,128)S(1)}, f32[576,256]{1,0:T(8,128)}, u32[]{:S(2)}) copy-start(f32[576,256]{1,0:T(8,128)} %bitcast_add_fusion.2) | copy-start | bytes 1769476
  232.6 10.1 %copy-start.5 = (f32[4,256,144]{1,2,0:T(8,128)}, f32[4,256,144]{1,2,0:T(8,128)S(1)}, u32[]{:S(2)}) copy-start(f32[4,256,144]{1,2,0:T(8,128)S(1)} %fusion.54) | copy-start | bytes 1769476
  241.8 1.5 copy-start.20
  241.8 1.5 copy-start.18
  243.4 55.4 %copy-start.4 = (f32[4,256,144]{1,2,0:T(8,128)S(1)}, f32[4,256,144]{1,2,0:T(8,128)}, u32[]{:S(2)}) copy-start(f32[4,256,144]{1,2,0:T(8,128)} %copy-done.3) | copy-start | bytes 1769476
  243.4 55.4 %copy-start.6 = (f32[4,256,144]{1,2,0:T(8,128)S(1)}, f32[4,256,144]{1,2,0:T(8,128)}, u32[]{:S(2)}) copy-start(f32[4,256,144]{1,2,0:T(8,128)} %copy-done.5) | copy-start | bytes 1769476
  243.4 55.4 %copy-start.12 = (f32[256]{0:T(256)S(1)}, f32[256]{0:T(256)}, u32[]{:S(2)}) copy-start(f32[256]{0:T(256)} %copy-done.11) | copy-start | bytes 3076
  243.4 55.4 %copy-start.14 = (f32[256]{0:T(256)S(1)}, f32[256]{0:T(256)}, u32[]{:S(2)}) copy-start(f32[256]{0:T(256)} %copy-done.13) | copy-start | bytes 3076
  280.2 17.8 %copy-start.21 = (f32[256]{0:T(256)S(1)}, f32[256]{0:T(256)}, u32[]{:S(2)}) copy-start(f32[256]{0:T(256)} %copy-done.20) | copy-start | bytes 3076
  298.8 11.0 %copy-start.19 = (f32[256]{0:T(256)}, f32[256]{0:T(256)S(1)}, u32[]{:S(2)}) copy-start(f32[256]{0:T(256)S(1)} %div.45) | copy-start | bytes 3076
  298.8 11.1 %copy-start.10 = (f32[144]{0:T(256)S(1)}, f32[144]{0:T(256)}, u32[]{:S(2)}) copy-start(f32[144]{0:T(256)} %copy-done.9) | copy-start | bytes 1732
  311.3 14.3 %all-to-all-start.4 = ((f32[8,32,144]{2,1,0:T(8,128)}), f32[8,32,144]{2,1,0:T(8,128)S(1)}, u32[]{:S(2)}, u32[]{:S(2)}) async-start(f32[8,32,144]{2,1,0:T(8,128)} %fusion.36), calls=%async_computation.4 | async-start | bytes 524288 | tf_op jit(solution)/shard_map/all_to_all | solution.py:112
Sparse Core Ops, SparseCore 0:
  45.2 35.1 all-gather.4
  107.8 37.3 all-gather.6
  175.9 37.3 all-gather.8
  242.9 37.3 all-gather.10
where the time goes:
time: 334 us; the launch traced here: 333 us
  waiting for transfers between devices  170 us (51%)
  blocking collectives  72 us (22%)
  matrix products  41.6 us (12%)
  starting transfers between devices  18.5 us (6%)
  between operations  14.1 us (4%)
  other arithmetic  11.7 us (4%)
  local copies, waits for them, and re-layouts  4.99 us (1%)
    all_gather x4, waiting for transfers between devices, shards(): lax.all_gather(direction, 'sub', axis=0, tiled=True)  147 us
    psum x4, blocking collectives, global_norm(): return lax.psum(column_sum(resid, zvec), 'sub')  35.9 us
    dot_general x4, matrix products, shards(): jnp.dot(matrix, lax.all_gather(direction, 'sub', axis=0, tiled=True), pre...  32.9 us
    psum x3, blocking collectives, shards(): alpha = rz_now / lax.psum(column_sum(direction, image), 'sub')  27.4 us
    all_to_all x1, blocking collectives, shards(): lax.all_to_all(reply, 'sub', split_axis=0, concat_axis=0, tiled=True)  8.69 us
    all_to_all x1, waiting for transfers between devices, shards(): lax.all_to_all(gathered, 'owner', split_axis=0, concat_axis=1, tiled=True)  8.21 us
    all_to_all x1, waiting for transfers between devices, shards(): lax.all_to_all(residual, 'owner', split_axis=1, concat_axis=0, tiled=True)  6.72 us
  transfers between devices with their start and end apart: 8, of which 8 were waited for; matrix products, arithmetic and copies ran while one was open for 2% of the time, Pallas kernels for 0%

commit v1 on v0

v1 whole, which is shorter than its diff:
```python
import functools

import jax
import jax.numpy as jnp
from jax import lax
from jax.experimental import pallas as pl
from jax.experimental.pallas import tpu as pltpu
from jax.sharding import PartitionSpec as P

ITERS = 4
LANES = 128
MESH = pl.DeviceIdType.MESH
F32 = jnp.float32
BF16 = jnp.bfloat16


def split(value):
    high = value.astype(BF16)
    return high, (value - high.astype(F32)).astype(BF16)


def split_cat(value):
    return jnp.concatenate(split(value), axis=1)


def fold(value):
    return value[:, :LANES] + value[:, LANES:]


def rows8(value):
    return jnp.sum(value.reshape(value.shape[0] // 8, 8, value.shape[1]), axis=0)


def dot(left, right):
    return jnp.dot(left, right, preferred_element_type=F32)


def total(acc):
    return jnp.sum(acc, axis=0, keepdims=True)


def kernel(
    dims,
    res_ref,
    trow_ref,
    tcol_ref,
    binv_ref,
    corner_ref,
    mat_hbm,
    corr_out,
    resid_out,
    mat,
    mat_hi,
    mat_lo,
    pcat,
    pvec,
    xvec,
    rvec,
    zvec,
    wbuf,
    wlast,
    inv_buf,
    cor_buf,
    inv_hi,
    inv_lo,
    tbuf,
    send_pieces,
    recv_pieces,
    lbuf,
    lcat,
    xcat,
    pick,
    pw_buf,
    corr_pieces,
    corr_back,
    mat_sem,
    sub_send,
    sub_recv,
    small_send,
    small_recv,
    own_send,
    own_recv,
):
    no, ns, rows, width, block, local, rhs = dims
    chunks = rhs // LANES
    nblk = width // block
    per = rows // block
    tail = block - LANES
    quota = rhs // no
    mo = lax.axis_index("owner")
    me = lax.axis_index("sub")
    relay = ns == 4
    pending = []

    def at(ref, start, size):
        return ref.at[pl.ds(pl.multiple_of(start, 8), size)]

    def remote(src, dst, ssem, rsem, where):
        return pltpu.make_async_remote_copy(
            src_ref=src, dst_ref=dst, send_sem=ssem, recv_sem=rsem, device_id=where,
            device_id_type=MESH,
        )

    mat_copy = pltpu.make_async_copy(mat_hbm.at[0], mat, mat_sem)
    mat_copy.start()

    barrier = pltpu.get_barrier_semaphore()
    for step in range(1, ns):
        pl.semaphore_signal(
            barrier, inc=1, device_id={"sub": lax.rem(me + step, ns)}, device_id_type=MESH
        )
    for step in range(1, no):
        pl.semaphore_signal(
            barrier, inc=1, device_id={"owner": lax.rem(mo + step, no)}, device_id_type=MESH
        )

    piece = local
    for part in range(no):
        send_pieces[part * quota : (part + 1) * quota, :] = res_ref[
            :, part * piece : (part + 1) * piece
        ]
    pl.semaphore_wait(barrier, ns - 1 + no - 1)

    class Gather:
        def __init__(self, index, buf, size, src=None):
            self.index, self.buf, self.size, self.src = index, buf, size, src
            self.copies = []

        def own(self, start, size):
            if self.src is not None:
                return self.src.at[pl.ds(start, size)]
            return at(self.buf, me * self.size + start, size)

        def add(self, kind, src, dst, peer):
            copy = remote(
                src, dst, sub_send.at[self.index, kind], sub_recv.at[self.index, kind],
                {"sub": peer},
            )
            copy.start()
            self.copies.append(copy)
            pending.append(copy)

        def start(self):
            size = self.size
            if relay:
                half = size // 2
                xn = me + 1 - 2 * lax.rem(me, 2)
                yn = lax.rem(me + 2, ns)
                self.xn, self.yn, self.half = xn, yn, half
                for kind, (peer, part) in enumerate(((xn, 0), (yn, 1), (xn, 1), (yn, 0))):
                    self.add(
                        kind, self.own(part * half, half),
                        at(self.buf, me * size + part * half, half), peer,
                    )
            else:
                for step in range(1, ns):
                    self.add(
                        step - 1, self.own(0, size), at(self.buf, me * size, size),
                        lax.rem(me + step, ns),
                    )

        def forward(self):
            if relay:
                size, half = self.size, self.half
                self.copies[0].wait_recv()
                first = at(self.buf, self.xn * size, half)
                self.add(4, first, first, self.yn)
                self.copies[1].wait_recv()
                second = at(self.buf, self.yn * size + half, half)
                self.add(5, second, second, self.xn)

        def finish(self):
            for copy in self.copies[2:] if relay else self.copies:
                copy.wait_recv()

    def small_gather(index, buf, size):
        copies = []
        for step in range(1, ns):
            mine = at(buf, me * size, size)
            copy = remote(
                mine, mine, small_send.at[index, step - 1], small_recv.at[index, step - 1],
                {"sub": lax.rem(me + step, ns)},
            )
            copy.start()
            copies.append(copy)
            pending.append(copy)
        return copies

    def exchange(index, src, dst):
        copies = []
        for step in range(1, no):
            peer = lax.rem(mo + step, no)
            copy = remote(
                at(src, peer * quota, quota), at(dst, mo * quota, quota),
                own_send.at[index, step - 1], own_recv.at[index, step - 1], {"owner": peer},
            )
            copy.start()
            copies.append(copy)
            pending.append(copy)
        mine = pl.ds(pl.multiple_of(mo * quota, 8), quota)
        dst[mine, :] = src[mine, :]
        return copies

    routed = exchange(0, send_pieces, recv_pieces)
    tbuf[pl.ds(pl.multiple_of(me * 8, 8), 8), :] = trow_ref[...]
    targets = small_gather(0, tbuf, 8)
    inv_gather = Gather(0, inv_buf, rows, binv_ref)
    inv_gather.start()
    cor_buf[pl.ds(pl.multiple_of(me * per * tail, 8), per * tail), :] = corner_ref[...]
    corners = small_gather(1, cor_buf, per * tail)
    inv_buf[pl.ds(pl.multiple_of(me * rows, 8), rows), :] = binv_ref[...]

    for copy in routed:
        copy.wait_recv()
    for c in range(chunks):
        lbuf[pl.ds(pl.multiple_of(me * local, 8), local), c * LANES : (c + 1) * LANES] = (
            recv_pieces[c * LANES : (c + 1) * LANES, :].T
        )
    local_gather = Gather(1, lbuf, local)
    local_gather.start()

    mat_copy.wait()
    strip = 48

    @pl.loop(0, rows // strip)
    def _(t):
        here = pl.ds(pl.multiple_of(t * strip, strip), strip)
        high, low = split(mat[here, :])
        mat_hi[here, :] = high
        mat_lo[here, :] = low

    for lane in range(0, width, 2 * LANES):
        spot = lax.broadcasted_iota(jnp.int32, (local, 2 * LANES), 1).astype(F32) + float(lane)
        pick[:, lane : lane + 2 * LANES] = jnp.where(spot == tcol_ref[...], 1.0, 0.0).astype(BF16)

    inv_gather.forward()
    local_gather.forward()
    for copy in corners:
        copy.wait_recv()
    inv_gather.finish()

    @pl.loop(0, nblk)
    def _(b):
        rows_b = inv_buf[pl.ds(pl.multiple_of(b * block, block), block), :]
        corner = cor_buf[pl.ds(pl.multiple_of(b * tail, tail), tail), :][:, :tail]
        right = jnp.concatenate([rows_b[LANES:, :].T, corner], axis=0)
        full = jnp.concatenate([rows_b, right], axis=1)
        high, low = split(full)
        inv_hi[b] = high
        inv_lo[b] = low

    for copy in targets:
        copy.wait_recv()
    local_gather.finish()

    @pl.loop(0, ns)
    def _(s):
        here = pl.ds(pl.multiple_of(s * local, local), local)
        for c in range(chunks):
            lcat[here, 2 * c * LANES : 2 * (c + 1) * LANES] = split_cat(
                lbuf[here, c * LANES : (c + 1) * LANES]
            )

    @pl.loop(0, nblk)
    def _(b):
        here = pl.ds(pl.multiple_of(b * block, block), block)
        spot = (lax.broadcasted_iota(jnp.int32, (block, local), 0) + b * block).astype(F32)
        acc = jnp.zeros((block, 2 * rhs), F32)
        for s in range(ns):
            hot = jnp.where(spot == tbuf[s * 8 : s * 8 + 1, :], 1.0, 0.0).astype(BF16)
            acc += dot(hot, lcat[s * local : (s + 1) * local, :])
        for c in range(chunks):
            rvec[c, here, :] = fold(acc[:, 2 * c * LANES : 2 * (c + 1) * LANES])

    group = 4 if nblk % 4 == 0 else 1

    def over_blocks(body):
        def step(t, acc):
            for u in range(group):
                b = t * group + u
                acc = acc + body(b, pl.ds(pl.multiple_of(b * block, block), block))
            return acc

        return lax.fori_loop(0, nblk // group, step, jnp.zeros((8, LANES), F32))

    def precond(b, resid):
        rcat = split_cat(resid)
        return fold(dot(inv_hi[b], rcat) + dot(inv_lo[b], rcat))

    tile = 2 * block if rows % (2 * block) == 0 else block

    def matvec(c, store):
        @pl.loop(0, rows // tile)
        def _(t):
            here = pl.ds(pl.multiple_of(t * tile, tile), tile)
            store(
                t * tile,
                fold(dot(mat_hi[here, :], pcat[c]) + dot(mat_lo[here, :], pcat[c])),
            )

    def send_image(step, c):
        def store(start, value):
            wbuf[step, c, pl.ds(pl.multiple_of(me * rows + start, 8), tile), :] = value

        matvec(c, store)
        gather = Gather(2 + step * chunks + c, wbuf.at[step, c], rows)
        gather.start()
        return gather

    def first(c):
        def body(b, here):
            resid = rvec[c, here, :]
            z = precond(b, resid)
            pvec[c, here, :] = z
            xvec[c, here, :] = jnp.zeros((block, LANES), F32)
            pcat[c, here, :] = split_cat(z)
            return rows8(resid * z)

        return total(over_blocks(body))

    def update(step, c, rz):
        pw = total(over_blocks(lambda b, here: rows8(pvec[c, here, :] * wbuf[step, c, here, :])))
        alpha = rz / pw

        def body(b, here):
            resid = rvec[c, here, :] - alpha * wbuf[step, c, here, :]
            rvec[c, here, :] = resid
            xvec[c, here, :] = xvec[c, here, :] + alpha * pvec[c, here, :]
            z = precond(b, resid)
            zvec[here, :] = z
            return rows8(resid * z)

        rz_next = total(over_blocks(body))
        beta = rz_next / rz

        @pl.loop(0, nblk)
        def _(b):
            here = pl.ds(pl.multiple_of(b * block, block), block)
            p = zvec[here, :] + beta * pvec[c, here, :]
            pvec[c, here, :] = p
            pcat[c, here, :] = split_cat(p)

        return rz_next

    rz, flight = [], []
    for c in range(chunks):
        rz.append(first(c))
        flight.append(send_image(0, c))

    sums = []
    for step in range(ITERS - 1):
        for c in range(chunks):
            flight[c].forward()
        for c in range(chunks):
            flight[c].finish()
            rz[c] = update(step, c, rz[c])
            if step < ITERS - 2:
                flight[c] = send_image(step + 1, c)
            else:

                def store(start, value, c=c):
                    wlast[c, pl.ds(pl.multiple_of(start, 8), tile), :] = value

                matvec(c, store)

                def partial(t, acc, c=c):
                    here = pl.ds(pl.multiple_of(t * block, block), block)
                    there = pl.ds(pl.multiple_of(me * rows + t * block, 8), block)
                    return acc + rows8(pvec[c, there, :] * wlast[c, here, :])

                pw_buf[c, pl.ds(pl.multiple_of(me * 8, 8), 8), :] = lax.fori_loop(
                    0, per, partial, jnp.zeros((8, LANES), F32)
                )
                sums.append(small_gather(2 + c, pw_buf.at[c], 8))

    for c in range(chunks):

        @pl.loop(0, nblk)
        def _(b, c=c):
            here = pl.ds(pl.multiple_of(b * block, block), block)
            xcat[here, :] = split_cat(xvec[c, here, :])

        base = fold(dot(pick[...], xcat[...]))
        slope = fold(dot(pick[...], pcat[c]))
        for copy in sums[c]:
            copy.wait_recv()
        alpha = rz[c] / total(rows8(pw_buf[c]))
        corr_pieces[c * LANES : (c + 1) * LANES, :] = (base + alpha * slope).T
        resid_out[0, :, c * LANES : (c + 1) * LANES] = (
            rvec[c, pl.ds(pl.multiple_of(me * rows, 8), rows), :] - alpha * wlast[c]
        )
    back = exchange(1, corr_pieces, corr_back)
    for copy in back:
        copy.wait_recv()
    for part in range(no):
        corr_out[:, part * piece : (part + 1) * piece] = corr_back[
            part * quota : (part + 1) * quota, :
        ]
    for copy in pending:
        copy.wait_send()


def shards(no, ns, residual, counts, assembly, level_two, block_inverse):
    _, slots, prim, width = assembly.shape
    rows = level_two.shape[1]
    block = block_inverse.shape[2]
    local = slots * prim
    quota = residual.shape[0]
    rhs = quota * no
    chunks = rhs // LANES
    nblk = width // block
    per = rows // block
    tail = block - LANES
    live = lax.broadcasted_iota(jnp.int32, (slots, prim), 1) < counts[0][:, None]
    flat = assembly[0]
    spot = jnp.sum(flat * lax.broadcasted_iota(jnp.int32, flat.shape, 2), axis=2)
    target = jnp.where(live, spot, -1).astype(F32).reshape(local)
    trow = jnp.broadcast_to(target[None, :], (8, local))
    tcol = target[:, None]
    inverse = block_inverse[0]
    corner = inverse.reshape(per, block, block)[:, LANES:, LANES:].reshape(per * tail, tail)
    corner = jnp.pad(corner, ((0, 0), (0, LANES - tail)))
    kinds = 6 if ns == 4 else ns - 1
    vmem = pl.BlockSpec(memory_space=pltpu.VMEM)
    dma = pltpu.SemaphoreType.DMA
    dims = (no, ns, rows, width, block, local, rhs)
    return pl.pallas_call(
        functools.partial(kernel, dims),
        out_shape=(
            jax.ShapeDtypeStruct(residual.shape, F32),
            jax.ShapeDtypeStruct((1, rows, rhs), F32),
        ),
        in_specs=[vmem] * 5 + [pl.BlockSpec(memory_space=pl.ANY)],
        out_specs=(vmem, vmem),
        scratch_shapes=[
            pltpu.VMEM((rows, width), F32),
            pltpu.VMEM((rows, width), BF16),
            pltpu.VMEM((rows, width), BF16),
            pltpu.VMEM((chunks, width, 2 * LANES), BF16),
            pltpu.VMEM((chunks, width, LANES), F32),
            pltpu.VMEM((chunks, width, LANES), F32),
            pltpu.VMEM((chunks, width, LANES), F32),
            pltpu.VMEM((width, LANES), F32),
            pltpu.VMEM((ITERS - 1, chunks, width, LANES), F32),
            pltpu.VMEM((chunks, rows, LANES), F32),
            pltpu.VMEM((width, LANES), F32),
            pltpu.VMEM((nblk * tail, LANES), F32),
            pltpu.VMEM((nblk, block, block), BF16),
            pltpu.VMEM((nblk, block, block), BF16),
            pltpu.VMEM((ns * 8, local), F32),
            pltpu.VMEM((rhs, local), F32),
            pltpu.VMEM((rhs, local), F32),
            pltpu.VMEM((ns * local, rhs), F32),
            pltpu.VMEM((ns * local, 2 * rhs), BF16),
            pltpu.VMEM((width, 2 * LANES), BF16),
            pltpu.VMEM((local, width), BF16),
            pltpu.VMEM((chunks, ns * 8, LANES), F32),
            pltpu.VMEM((rhs, local), F32),
            pltpu.VMEM((rhs, local), F32),
            dma,
            dma((2 + (ITERS - 1) * chunks, kinds)),
            dma((2 + (ITERS - 1) * chunks, kinds)),
            dma((2 + chunks, ns - 1)),
            dma((2 + chunks, ns - 1)),
            dma((2, no - 1)),
            dma((2, no - 1)),
        ],
        compiler_params=pltpu.CompilerParams(
            collective_id=0, has_side_effects=True, vmem_limit_bytes=60 * 1024 * 1024
        ),
    )(residual, trow, tcol, inverse[:, :LANES], corner, level_two)


def solution(mesh):
    in_specs = (
        P("owner", "sub"),
        P("owner", "sub"),
        P("owner", "sub", None, None),
        P("owner", "sub", None),
        P("owner", "sub", None),
    )
    out_specs = (P("owner", "sub"), P("owner", "sub", None))
    body = functools.partial(shards, mesh.shape["owner"], mesh.shape["sub"])
    return jax.shard_map(body, mesh=mesh, in_specs=in_specs, out_specs=out_specs, check_vma=False)
```

time: 334 us -> 117 us (0.35)
  waiting for transfers between devices: 170 us -> 0 us
  Pallas kernels: 0 us -> 108 us
  blocking collectives: 72 us -> 0 us
  matrix products: 41.6 us -> 0 us
  starting transfers between devices: 18.5 us -> 0 us
  between operations: 14.1 us -> 0.68 us
  other arithmetic: 11.7 us -> 2.15 us
    all_gather x4 -> x0, waiting for transfers between devices: 147 us -> none  [shards(): lax.all_gather(direction, 'sub', axis=0, tiled=True)]
    pallas_call x0 -> x1, Pallas kernels: none -> 108 us  [shards(): pl.pallas_call(functools.partial(kernel, dims), out_shape=(jax.ShapeDtype...]
    psum x7 -> x0, blocking collectives: 63.3 us -> none  [the longest x4 35.9 us: global_norm(): return lax.psum(column_sum(resid, zvec), 'sub')]
    dot_general x13 -> x0, matrix products: 41.6 us -> none  [the longest x4 32.9 us: shards(): jnp.dot(matrix, lax.all_gather(direction, 'sub', axis=0, tiled=True), pre...]
    all_to_all x4 -> x0, waiting for transfers between devices: 23.4 us -> none  [the longest x1 8.21 us: shards(): lax.all_to_all(gathered, 'owner', split_axis=0, concat_axis=1, tiled=True)]
    all_to_all x4 -> x0, starting transfers between devices: 18.1 us -> none  [the longest x1 6.35 us: shards(): lax.all_to_all(residual, 'owner', split_axis=1, concat_axis=0, tiled=True)]
    all_to_all x1 -> x0, blocking collectives: 8.69 us -> none  [shards(): lax.all_to_all(reply, 'sub', split_axis=0, concat_axis=0, tiled=True)]
    add x6 -> x0, other arithmetic: 3.64 us -> none  [the longest x3 2.67 us: shards(): direction = zvec + rz_next / rz_now * direction]
  transfers between devices with their start and end apart: 8 -> 0, of which waited for: 8 -> 0; matrix products, arithmetic and copies ran while one was open for 2% -> 0% of each run, Pallas kernels for 0% -> 0%
where the time goes in v1:
time: 117 us
  Pallas kernels  108 us (92%)
  local copies, waits for them, and re-layouts  6.57 us (6%)
  other arithmetic  2.15 us (2%)
    pallas_call x1, Pallas kernels, shards(): pl.pallas_call(functools.partial(kernel, dims), out_shape=(jax.ShapeDtype...  108 us
    unnamed x7, local copies, waits for them, and re-layouts  3.72 us

profile of v1, /device:TPU:0, one launch (start us, length us, event | category | flops | bytes accessed | tf_op | source)
XLA Modules:
  0.0 117.1 jit_solution(8382627281777482043)
XLA Ops:
  0.6 0.0 copy-start
  0.6 0.0 copy-start.1
  0.7 2.1 %fusion = s32[4,36]{0,1:T(8,128)S(1)} fusion(s32[1,4,36,2304]{3,1,2,0:T(4,128)} %param.7), kind=kLoop, calls=%fused_computation.1 | loop fusion | flops 663408 | bytes 1327680 | tf_op jit(solution)/shard_map/reduce_sum | solution.py:416
  2.7 0.1 copy.21
  2.8 0.0 copy-done.1
  2.8 0.1 select_convert_fusion
  2.9 0.1 convert_element_type.23
  3.0 0.6 broadcast_in_dim.10.trow_ref
  3.6 0.7 convert_element_type.25.tcol_ref
  4.3 0.0 copy-done
  4.3 0.2 copy.22
  4.6 0.6 pad.4.corner_ref
  5.2 0.7 slice.8.binv_ref
  5.9 107.7 %shard_map.68 = (f32[32,1152]{1,0:T(8,128)}, f32[1,576,256]{2,1,0:T(8,128)}) custom-call(f32[32,1152]{1,0:T(8,128)} %res_ref.1, f32[8,144]{1,0:T(8,128)} %broadcast_in_dim.10.trow_ref, f32[144,1]{1,0:T(8,128)} %convert_element_type.25.tcol_ref, f32[576,128]{1,0:T(8,128)} %slice.8.binv_ref, f32[64,128]{1,0:T(8,128)} %pad.4.corner_ref, f32[1,576,2304]{2,1,0:T(8,128)} %mat_hbm.1), custom_call_target="tpu_custom_call" | custom-call | tf_op jit(solution)/shard_map/pallas_call | solution.py:427
  113.6 1.6 %copy.28 = f32[32,1152]{1,0:T(8,128)} copy(f32[32,1152]{1,0:T(8,128)} %get-tuple-element.4) | data formatting | bytes 294912
  115.2 1.9 %copy.29 = f32[1,576,256]{2,1,0:T(8,128)} copy(f32[1,576,256]{2,1,0:T(8,128)} %get-tuple-element.5) | data formatting | bytes 1179648
  (1 shorter events, 0.0 us)
Async XLA Ops:
  0.6 3.7 %copy-start = (f32[1,576,144]{1,2,0:T(8,128)S(1)}, f32[1,576,144]{1,2,0:T(8,128)}, u32[]{:S(2)}) copy-start(f32[1,576,144]{1,2,0:T(8,128)} %param.9) | copy-start | bytes 995332
  0.6 2.2 %copy-start.1 = (s32[1,4]{1,0:T(1,128)S(1)}, s32[1,4]{1,0:T(1,128)}, u32[]{:S(2)}) copy-start(s32[1,4]{1,0:T(1,128)} %param.6) | copy-start | bytes 52

commit v2 on v1

--- a/solution.py
+++ b/solution.py
@@ -42,10 +42,9 @@
 def kernel(
     dims,
     res_ref,
-    trow_ref,
-    tcol_ref,
-    binv_ref,
-    corner_ref,
+    counts_ref,
+    hot_hbm,
+    inv_hbm,
     mat_hbm,
     corr_out,
     resid_out,
@@ -73,7 +72,12 @@
     pw_buf,
     corr_pieces,
     corr_back,
+    inv_own,
+    hot_own,
+    tcol,
     mat_sem,
+    inv_sem,
+    hot_sem,
     sub_send,
     sub_recv,
     small_send,
@@ -102,6 +106,16 @@
         )
 
     mat_copy = pltpu.make_async_copy(mat_hbm.at[0], mat, mat_sem)
+    inv_copies = [
+        pltpu.make_async_copy(
+            inv_hbm.at[0, :, pl.ds(0, LANES)], at(inv_buf, me * rows, rows), inv_sem.at[0]
+        ),
+        pltpu.make_async_copy(inv_hbm.at[0], inv_own, inv_sem.at[1]),
+    ]
+    hot_copy = pltpu.make_async_copy(hot_hbm.at[0], hot_own, hot_sem)
+    for copy in inv_copies:
+        copy.start()
+    hot_copy.start()
     mat_copy.start()
 
     barrier = pltpu.get_barrier_semaphore()
@@ -202,13 +216,31 @@
         return copies
 
     routed = exchange(0, send_pieces, recv_pieces)
-    tbuf[pl.ds(pl.multiple_of(me * 8, 8), 8), :] = trow_ref[...]
+    inv_copies[0].wait()
+    inv_gather = Gather(0, inv_buf, rows)
+    inv_gather.start()
+    inv_copies[1].wait()
+    for q in range(per):
+        corner_own = inv_own[q * block + LANES : (q + 1) * block, :][:, LANES:]
+        cor_buf[pl.ds(pl.multiple_of((me * per + q) * tail, 8), tail), :] = jnp.concatenate(
+            [corner_own, jnp.zeros((tail, LANES - tail), F32)], axis=1
+        )
+    corners = small_gather(1, cor_buf, per * tail)
+
+    hot_copy.wait()
+    slots, prim = hot_own.shape[0], hot_own.shape[1]
+    for q in range(slots):
+        acc = jnp.zeros((prim, LANES), F32)
+        spot = lax.broadcasted_iota(jnp.int32, (prim, LANES), 1)
+        for lane in range(0, width, LANES):
+            acc += (hot_own[q, :, lane : lane + LANES] * (spot + lane)).astype(F32)
+        value = jnp.sum(acc, axis=1, keepdims=True)
+        alive = lax.broadcasted_iota(jnp.int32, (prim, 1), 0) < counts_ref[0, q]
+        tcol[q * prim : (q + 1) * prim, :] = jnp.broadcast_to(
+            jnp.where(alive, value, -1.0), (prim, LANES)
+        )
+    tbuf[pl.ds(pl.multiple_of(me * 8, 8), 8), :] = tcol[...].T[:8, :]
     targets = small_gather(0, tbuf, 8)
-    inv_gather = Gather(0, inv_buf, rows, binv_ref)
-    inv_gather.start()
-    cor_buf[pl.ds(pl.multiple_of(me * per * tail, 8), per * tail), :] = corner_ref[...]
-    corners = small_gather(1, cor_buf, per * tail)
-    inv_buf[pl.ds(pl.multiple_of(me * rows, 8), rows), :] = binv_ref[...]
 
     for copy in routed:
         copy.wait_recv()
@@ -231,7 +263,7 @@
 
     for lane in range(0, width, 2 * LANES):
         spot = lax.broadcasted_iota(jnp.int32, (local, 2 * LANES), 1).astype(F32) + float(lane)
-        pick[:, lane : lane + 2 * LANES] = jnp.where(spot == tcol_ref[...], 1.0, 0.0).astype(BF16)
+        pick[:, lane : lane + 2 * LANES] = jnp.where(spot == tcol[:, :1], 1.0, 0.0).astype(BF16)
 
     inv_gather.forward()
     local_gather.forward()
@@ -298,11 +330,13 @@
                 fold(dot(mat_hi[here, :], pcat[c]) + dot(mat_lo[here, :], pcat[c])),
             )
 
-    def send_image(step, c):
+    def send_image(step, c, earlier):
         def store(start, value):
             wbuf[step, c, pl.ds(pl.multiple_of(me * rows + start, 8), tile), :] = value
 
         matvec(c, store)
+        if earlier is not None:
+            earlier.forward()
         gather = Gather(2 + step * chunks + c, wbuf.at[step, c], rows)
         gather.start()
         return gather
@@ -342,53 +376,59 @@
 
         return rz_next
 
-    rz, flight = [], []
+    rz, flight, earlier = [], [], None
     for c in range(chunks):
         rz.append(first(c))
-        flight.append(send_image(0, c))
-
-    sums = []
-    for step in range(ITERS - 1):
-        for c in range(chunks):
-            flight[c].forward()
+        earlier = send_image(0, c, earlier)
+        flight.append(earlier)
+
+    for step in range(ITERS - 2):
         for c in range(chunks):
             flight[c].finish()
             rz[c] = update(step, c, rz[c])
-            if step < ITERS - 2:
-                flight[c] = send_image(step + 1, c)
-            else:
-
-                def store(start, value, c=c):
-                    wlast[c, pl.ds(pl.multiple_of(start, 8), tile), :] = value
-
-                matvec(c, store)
-
-                def partial(t, acc, c=c):
-                    here = pl.ds(pl.multiple_of(t * block, block), block)
-                    there = pl.ds(pl.multiple_of(me * rows + t * block, 8), block)
-                    return acc + rows8(pvec[c, there, :] * wlast[c, here, :])
-
-                pw_buf[c, pl.ds(pl.multiple_of(me * 8, 8), 8), :] = lax.fori_loop(
-                    0, per, partial, jnp.zeros((8, LANES), F32)
-                )
-                sums.append(small_gather(2 + c, pw_buf.at[c], 8))
-
-    for c in range(chunks):
-
-        @pl.loop(0, nblk)
-        def _(b, c=c):
-            here = pl.ds(pl.multiple_of(b * block, block), block)
-            xcat[here, :] = split_cat(xvec[c, here, :])
-
-        base = fold(dot(pick[...], xcat[...]))
-        slope = fold(dot(pick[...], pcat[c]))
-        for copy in sums[c]:
+            earlier = send_image(step + 1, c, earlier)
+            flight[c] = earlier
+
+    def conclude(c, sums, base, slope):
+        for copy in sums:
             copy.wait_recv()
         alpha = rz[c] / total(rows8(pw_buf[c]))
         corr_pieces[c * LANES : (c + 1) * LANES, :] = (base + alpha * slope).T
         resid_out[0, :, c * LANES : (c + 1) * LANES] = (
             rvec[c, pl.ds(pl.multiple_of(me * rows, 8), rows), :] - alpha * wlast[c]
         )
+
+    for c in range(chunks):
+        if c == chunks - 1 and chunks == 1:
+            earlier.forward()
+        flight[c].finish()
+        rz[c] = update(ITERS - 2, c, rz[c])
+        if c == chunks - 2:
+            earlier.forward()
+
+        def store(start, value, c=c):
+            wlast[c, pl.ds(pl.multiple_of(start, 8), tile), :] = value
+
+        matvec(c, store)
+
+        def partial(t, acc, c=c):
+            here = pl.ds(pl.multiple_of(t * block, block), block)
+            there = pl.ds(pl.multiple_of(me * rows + t * block, 8), block)
+            return acc + rows8(pvec[c, there, :] * wlast[c, here, :])
+
+        pw_buf[c, pl.ds(pl.multiple_of(me * 8, 8), 8), :] = lax.fori_loop(
+            0, per, partial, jnp.zeros((8, LANES), F32)
+        )
+        sums = small_gather(2 + c, pw_buf.at[c], 8)
+
+        @pl.loop(0, nblk)
+        def _(b, c=c):
+            here = pl.ds(pl.multiple_of(b * block, block), block)
+            xcat[here, :] = split_cat(xvec[c, here, :])
+
+        base = fold(dot(pick[...], xcat[...]))
+        slope = fold(dot(pick[...], pcat[c]))
+        conclude(c, sums, base, slope)
     back = exchange(1, corr_pieces, corr_back)
     for copy in back:
         copy.wait_recv()
@@ -411,15 +451,6 @@
     nblk = width // block
     per = rows // block
     tail = block - LANES
-    live = lax.broadcasted_iota(jnp.int32, (slots, prim), 1) < counts[0][:, None]
-    flat = assembly[0]
-    spot = jnp.sum(flat * lax.broadcasted_iota(jnp.int32, flat.shape, 2), axis=2)
-    target = jnp.where(live, spot, -1).astype(F32).reshape(local)
-    trow = jnp.broadcast_to(target[None, :], (8, local))
-    tcol = target[:, None]
-    inverse = block_inverse[0]
-    corner = inverse.reshape(per, block, block)[:, LANES:, LANES:].reshape(per * tail, tail)
-    corner = jnp.pad(corner, ((0, 0), (0, LANES - tail)))
     kinds = 6 if ns == 4 else ns - 1
     vmem = pl.BlockSpec(memory_space=pltpu.VMEM)
     dma = pltpu.SemaphoreType.DMA
@@ -430,7 +461,8 @@
             jax.ShapeDtypeStruct(residual.shape, F32),
             jax.ShapeDtypeStruct((1, rows, rhs), F32),
         ),
-        in_specs=[vmem] * 5 + [pl.BlockSpec(memory_space=pl.ANY)],
+        in_specs=[vmem, pl.BlockSpec(memory_space=pltpu.SMEM)]
+        + [pl.BlockSpec(memory_space=pl.ANY)] * 3,
         out_specs=(vmem, vmem),
         scratch_shapes=[
             pltpu.VMEM((rows, width), F32),
@@ -457,6 +489,11 @@
             pltpu.VMEM((chunks, ns * 8, LANES), F32),
             pltpu.VMEM((rhs, local), F32),
             pltpu.VMEM((rhs, local), F32),
+            pltpu.VMEM((rows, block), F32),
+            pltpu.VMEM((slots, prim, width), jnp.int32),
+            pltpu.VMEM((local, LANES), F32),
+            dma,
+            dma((2,)),
             dma,
             dma((2 + (ITERS - 1) * chunks, kinds)),
             dma((2 + (ITERS - 1) * chunks, kinds)),
@@ -468,7 +505,7 @@
         compiler_params=pltpu.CompilerParams(
             collective_id=0, has_side_effects=True, vmem_limit_bytes=60 * 1024 * 1024
         ),
-    )(residual, trow, tcol, inverse[:, :LANES], corner, level_two)
+    )(residual, counts, assembly, block_inverse, level_two)
 
 
 def solution(mesh):

time: 117 us -> 114 us (0.974)
  Pallas kernels: 108 us -> 105 us
  other arithmetic: 2.15 us -> 0 us
  local copies, waits for them, and re-layouts: 6.57 us -> 8.25 us
    unnamed x7 -> x4, local copies, waits for them, and re-layouts: 3.72 us -> 8.25 us
    pallas_call x1, Pallas kernels: 108 us -> 105 us  [shards(): pl.pallas_call(functools.partial(kernel, dims), out_shape=(jax.ShapeDtype...]
    reduce_sum x1 -> x0, other arithmetic: 2.08 us -> none  [shards(): jnp.sum(flat * lax.broadcasted_iota(jnp.int32, flat.shape, 2), axis=2)]
where the time goes in v2:
time: 114 us
  Pallas kernels  105 us (92%)
  local copies, waits for them, and re-layouts  8.25 us (7%)
    pallas_call x1, Pallas kernels, shards(): pl.pallas_call(functools.partial(kernel, dims), out_shape=(jax.ShapeDtype...  105 us
    unnamed x4, local copies, waits for them, and re-layouts  8.25 us

profile of v2, /device:TPU:0, one launch (start us, length us, event | category | flops | bytes accessed | tf_op | source)
XLA Modules:
  0.0 113.7 jit_solution(10696662096931199188)
XLA Ops:
  0.6 2.0 %copy.8.inv_hbm = f32[1,576,144]{2,1,0:T(8,128)} copy(f32[1,576,144]{1,2,0:T(8,128)} %param.9) | data formatting | bytes 663552 | tf_op args[4]
  2.7 2.7 %copy.7.hot_hbm = s32[1,4,36,2304]{3,2,1,0:T(8,128)} copy(s32[1,4,36,2304]{3,1,2,0:T(4,128)} %param.7) | data formatting | bytes 2654208 | tf_op args[2]
  5.4 104.9 %shard_map.68 = (f32[32,1152]{1,0:T(8,128)}, f32[1,576,256]{2,1,0:T(8,128)}) custom-call(f32[32,1152]{1,0:T(8,128)} %res_ref.1, s32[1,4]{1,0:T(1,128)} %counts_ref.1, s32[1,4,36,2304]{3,2,1,0:T(8,128)} %copy.7.hot_hbm, f32[1,576,144]{2,1,0:T(8,128)} %copy.8.inv_hbm, f32[1,576,2304]{2,1,0:T(8,128)} %mat_hbm.1), custom_call_target="tpu_custom_call" | custom-call | tf_op jit(solution)/shard_map/pallas_call | solution.py:458
  110.2 1.6 %copy.11 = f32[32,1152]{1,0:T(8,128)} copy(f32[32,1152]{1,0:T(8,128)} %get-tuple-element.4) | data formatting | bytes 294912
  111.8 1.9 %copy.12 = f32[1,576,256]{2,1,0:T(8,128)} copy(f32[1,576,256]{2,1,0:T(8,128)} %get-tuple-element.5) | data formatting | bytes 1179648
